TPU v7x, 128 devices: a whole 4x4x4 slice. The times are simulated.
128 devices in a mesh: probe: 4 (over z_hi, core), fsdp: 32 (over y, z_lo, x).
Axes of the slice: x: 4, y: 4, z: 4 (z_hi: 2, z_lo: 2; z = z_hi * 2 + z_lo), core: 2. Of those that a mesh axis runs over, the one named last changes fastest.
Arguments:
- hidden: bfloat16 [65536, 2048], P(('probe', 'fsdp')), may hold values from -6 to 6
- norm_gain: bfloat16 [2048], replicated, may hold values from 0.5 to 1.5
- query_weight: bfloat16 [2048, 2048], P('fsdp'), may hold values from -1 to 1
- key_weight: bfloat16 [2048, 512], P('fsdp'), may hold values from -16 to 16
- value_weight: bfloat16 [2048, 512], P('fsdp'), may hold values from -0.125 to 0.125
- output_weight: bfloat16 [2048, 2048], P('fsdp'), may hold values from -0.125 to 0.125
- probe_seed: int32 [4], P('probe'), may hold values from 0 to 1073741823
Outputs:
- curvature_value: float32 [2048, 512], P('fsdp', 'probe')
- curvature_output: float32 [2048, 2048], P('fsdp', 'probe')
All inputs are finite; a program needn't handle non-finite values.
Results may differ from a plain program's by a relative error of at most 0.024.
Values may be sent and summed in bfloat16 or wider, within the bound.
No kernel may reach another device: no remote copies, remote signals or barrier semaphores. Data moves between devices by JAX's collectives and lax.ppermute only.
A program may use at most 128 MiB of HBM per device.

v0:
```python
import jax
import jax.numpy as jnp
from jax import lax
from jax.sharding import PartitionSpec as P

HEAD_DIM = 128
SEQ = 256
norm_eps = 1e-05
rope_base = 500000.0


def in_one_piece(arrays, axis, dim, along):
    both = jnp.concatenate(arrays, axis=along)
    result, at, finished = (lax.all_gather(both, axis, axis=dim, tiled=True), 0, [])
    for a in arrays:
        finished.append(lax.slice_in_dim(result, at, at + a.shape[along], axis=along))
        at += a.shape[along]
    return tuple(finished)


def split_up(value, dim, size):
    dims = value.shape
    parts = value.reshape(*dims[:dim], size, dims[dim] // size, *dims[dim + 1 :])
    return jnp.moveaxis(parts, dim, 0)


def sent_and_summed(value, axis, dim):
    size = lax.axis_size(axis)
    parts = lax.all_to_all(split_up(value, dim, size), axis, 0, 0, tiled=True)
    return jnp.sum(parts.astype(jnp.float32), axis=0)


def sign_table(seed_value, matrix_code, row_total, column_total):
    row_index = lax.broadcasted_iota(jnp.int32, (row_total, column_total), 0)
    column_index = lax.broadcasted_iota(jnp.int32, (row_total, column_total), 1)
    hashed = (row_index * column_total + column_index) * 747796405 + (
        seed_value * 1664525 + matrix_code * 374761393
    )
    hashed = hashed ^ lax.shift_right_logical(hashed, jnp.int32(15))
    hashed = hashed * 668265261
    hashed = hashed ^ lax.shift_right_logical(hashed, jnp.int32(13))
    hashed = hashed * 1274126177
    hashed = hashed ^ lax.shift_right_logical(hashed, jnp.int32(16))
    return jnp.where(hashed & 1 == 1, 1.0, -1.0).astype(jnp.bfloat16)


def normalize(rows_in, gain_row):
    values = rows_in.astype(jnp.float32)
    inverse = lax.rsqrt(jnp.mean(values * values, axis=1, keepdims=True) + norm_eps)
    return (values * inverse * gain_row.astype(jnp.float32)[None, :]).astype(jnp.bfloat16)


def rotate(projected, head_count):
    row_count = projected.shape[0]
    columns = projected.shape[1]
    head_size = columns // head_count
    half_dim = head_size // 2
    position = (lax.broadcasted_iota(jnp.int32, (row_count, 1), 0) % SEQ).astype(jnp.float32)
    exponent = lax.broadcasted_iota(jnp.int32, (1, half_dim), 1).astype(jnp.float32) * (
        -2.0 / head_size
    )
    frequency = jnp.power(jnp.float32(rope_base), exponent)
    angles = position * frequency
    cosine = jnp.cos(angles)[:, None, :]
    sine_part = jnp.sin(angles)[:, None, :]
    shaped = projected.reshape(row_count, head_count, head_size)
    leading = shaped[:, :, :half_dim]
    trailing = shaped[:, :, half_dim:]
    turned = jnp.concatenate(
        [leading * cosine - trailing * sine_part, trailing * cosine + leading * sine_part], axis=2
    )
    return turned.reshape(row_count, columns).astype(jnp.bfloat16)


def attend(query_rows, key_rows):
    row_count = query_rows.shape[0]
    key_heads = key_rows.shape[1] // HEAD_DIM
    group_size = query_rows.shape[1] // key_rows.shape[1]
    sequences = row_count // SEQ
    grouped_query = query_rows.reshape(sequences, SEQ, key_heads, group_size, HEAD_DIM)
    grouped_key = key_rows.reshape(sequences, SEQ, key_heads, HEAD_DIM)
    scores = jnp.einsum(
        "bqkgd,bskd->bkgqs", grouped_query, grouped_key, preferred_element_type=jnp.float32
    ) * HEAD_DIM ** (-0.5)
    causal_mask = lax.broadcasted_iota(jnp.int32, (SEQ, SEQ), 0) >= lax.broadcasted_iota(
        jnp.int32, (SEQ, SEQ), 1
    )
    scores = jnp.where(causal_mask, scores, -1e30)
    highest = jnp.max(scores, axis=4, keepdims=True)
    raised = jnp.exp(scores - highest)
    return (raised / jnp.sum(raised, axis=4, keepdims=True)).astype(jnp.bfloat16)


def mix_values(attention, value_rows):
    sequences = attention.shape[0]
    key_heads = attention.shape[1]
    group_size = attention.shape[2]
    grouped_value = value_rows.reshape(sequences, SEQ, key_heads, HEAD_DIM)
    combined = jnp.einsum(
        "bkgqs,bskd->bqkgd", attention, grouped_value, preferred_element_type=jnp.float32
    )
    return combined.reshape(sequences * SEQ, key_heads * group_size * HEAD_DIM)


def spread_back(attention, upstream):
    sequences = attention.shape[0]
    key_heads = attention.shape[1]
    group_size = attention.shape[2]
    grouped_upstream = upstream.reshape(sequences, SEQ, key_heads, group_size, HEAD_DIM)
    spread = jnp.einsum(
        "bkgqs,bqkgd->bskd", attention, grouped_upstream, preferred_element_type=jnp.float32
    )
    return spread.reshape(sequences * SEQ, key_heads * HEAD_DIM)


def body(hidden, norm_gain, query_weight, key_weight, value_weight, output_weight, probe_seed):
    seed_value = probe_seed[0]
    normed = normalize(hidden, norm_gain)
    model_width = normed.shape[1]
    query_width = query_weight.shape[1]
    key_width = key_weight.shape[1]
    head_count = query_width // HEAD_DIM
    key_heads = key_width // HEAD_DIM
    contract_rows = (((0,), (0,)), ((), ()))
    contract_columns = (((1,), (1,)), ((), ()))
    portions = in_one_piece((query_weight, key_weight, value_weight), "fsdp", 0, 1)
    query_raw = jnp.dot(normed, portions[0], preferred_element_type=jnp.float32)
    key_raw = jnp.dot(normed, portions[1], preferred_element_type=jnp.float32)
    value_raw = jnp.dot(normed, portions[2], preferred_element_type=jnp.float32)
    query_rows = rotate(query_raw, head_count)
    key_rows = rotate(key_raw, key_heads)
    value_rows = value_raw.astype(jnp.bfloat16)
    attention = attend(query_rows, key_rows)
    context = mix_values(attention, value_rows).astype(jnp.bfloat16)
    signs_value = sign_table(seed_value, 0, model_width, key_width)
    signs_out = sign_table(seed_value, 1, query_width, model_width)
    tangent_value = (
        jnp.dot(normed, signs_value, preferred_element_type=jnp.float32) * model_width ** (-0.5)
    ).astype(jnp.bfloat16)
    tangent_context = mix_values(attention, tangent_value).astype(jnp.bfloat16)
    probe_part = jnp.dot(context, signs_out, preferred_element_type=jnp.float32) * query_width ** (
        -0.5
    )
    whole_out = lax.all_gather(output_weight, "fsdp", axis=0, tiled=True)
    forward_part = jnp.dot(tangent_context, whole_out, preferred_element_type=jnp.float32)
    cotangent = (forward_part + probe_part).astype(jnp.bfloat16)
    back_context = lax.dot_general(
        cotangent, whole_out, contract_columns, preferred_element_type=jnp.float32
    )
    back_value = spread_back(attention, back_context.astype(jnp.bfloat16)).astype(jnp.bfloat16)
    portion = normed
    value_share = sent_and_summed(
        lax.dot_general(
            portion, back_value, contract_rows, preferred_element_type=jnp.float32
        ).astype(jnp.bfloat16),
        "fsdp",
        0,
    )
    portion = context
    output_share = lax.psum_scatter(
        lax.dot_general(
            portion, cotangent, contract_rows, preferred_element_type=jnp.float32
        ).astype(jnp.bfloat16),
        "fsdp",
        scatter_dimension=0,
        tiled=True,
    )
    curvature_value, curvature_output = (
        sent_and_summed(value_share.astype(jnp.bfloat16), "probe", 1),
        sent_and_summed(output_share, "probe", 1),
    )
    return (curvature_value, curvature_output)


def solution(mesh):
    return jax.shard_map(
        body,
        mesh=mesh,
        in_specs=(
            P(("probe", "fsdp"), None),
            P(),
            P("fsdp", None),
            P("fsdp", None),
            P("fsdp", None),
            P("fsdp", None),
            P("probe"),
        ),
        out_specs=(P("fsdp", "probe"), P("fsdp", "probe")),
        check_vma=False,
    )
```

profile of v0, /device:TPU:1, one launch (start us, length us, event | category | flops | bytes accessed | tf_op | source)
XLA Modules:
  0.0 591.7 jit_solution(6584148597963998947)
XLA Ops:
  13.3 4.8 fusion.63
  20.1 148.7 %all-gather.3.cloned.1.call-done = bf16[2048,3072]{1,0:T(8,128)(2,1)} async-done(((bf16[64,3072]{1,0:T(8,128)(2,1)}), bf16[2048,3072]{1,0:T(8,128)(2,1)}) %all-gather.3.cloned.1.call-update) | async-done | bytes 12582928 | tf_op jit(solution)/shard_map/all_gather | solution.py:14
  168.8 2.9 fusion.57
  172.7 7.5 %fusion.30 = f32[64,8,16,128]{3,1,2,0:T(8,128)S(1)} fusion(bf16[2048,3072]{1,0:T(8,128)(2,1)} %all-gather.3.cloned.1.call-done, bf16[512,2048]{1,0:T(8,128)(2,1)S(1)} %copy-done.2, f32[2048]{0:T(1024)S(1)} %convert_element_type.128, f32[512]{0:T(512)S(1)} %add_rsqrt_fusion), kind=kOutput, calls=%fused_computation.49 | convolution fusion | flops 4299161600 | bytes 14690304 | tf_op jit(solution)/shard_map/dot_general | solution.py:127
  180.2 2.9 copy.83
  183.1 3.0 fusion.36
  202.0 3.1 copy.59
  205.1 4.5 convert_element_type.143
  209.6 3.0 convert_bitcast_fusion.1
  212.6 3.1 copy.56
  215.7 4.5 convert_element_type.139
  220.2 113.2 %all-gather.5.cloned.1.call-done = bf16[2048,2048]{1,0:T(8,128)(2,1)} async-done(((bf16[64,2048]{1,0:T(8,128)(2,1)}), bf16[2048,2048]{1,0:T(8,128)(2,1)}) %all-gather.5.cloned.1.call-update) | async-done | bytes 8388624 | tf_op jit(solution)/shard_map/all_gather | solution.py:144
  333.4 7.8 %fusion.104 = f32[512,2048]{1,0:T(8,128)S(1)} fusion(bf16[512,2048]{1,0:T(8,128)(2,1)} %convert_element_type.139, bf16[2048,2048]{1,0:T(8,128)(2,1)} %all-gather.5.cloned.1.call-done), kind=kOutput, calls=%fused_computation.127 | convolution fusion | flops 4294967296 | bytes 14680064 | tf_op jit(solution)/shard_map/dot_general | solution.py:145
  341.2 10.0 %add_convert_fusion = bf16[512,2048]{1,0:T(8,128)(2,1)S(1)} fusion(f32[512,2048]{1,0:T(8,128)S(1)} %fusion.104, bf16[512,2048]{1,0:T(8,128)(2,1)S(1)} %copy-done.3, s32[]{:T(128)S(6)} %add.79, s32[2048]{0:T(1024)S(1)} %iota_multiply_fusion), kind=kOutput, calls=%fused_computation.40 | convolution fusion | flops 4361027584 | bytes 8396804 | tf_op jit(solution)/shard_map/dot_general | solution.py:141
  352.6 6.8 %convolution_convert_fusion = bf16[2048,2048]{1,0:T(8,128)(2,1)} fusion(bf16[512,2048]{1,0:T(8,128)(2,1)S(1)} %copy-done.3, bf16[512,2048]{1,0:T(8,128)(2,1)S(1)} %add_convert_fusion), kind=kOutput, calls=%fused_computation.26 | convolution fusion | flops 4299161600 | bytes 12582912 | tf_op jit(solution)/shard_map/dot_general | solution.py:161
  360.9 9.4 %convolution_convert_fusion.2 = bf16[512,2048]{1,0:T(8,128)(2,1)} fusion(bf16[512,2048]{1,0:T(8,128)(2,1)S(1)} %copy-done.7, bf16[2048,2048]{1,0:T(8,128)(2,1)} %all-gather.5.cloned.1.call-done), kind=kOutput, calls=%fused_computation.48 | convolution fusion | flops 4296015872 | bytes 12582912 | tf_op jit(solution)/shard_map/dot_general | solution.py:147
  370.3 3.2 reshape.132
  373.5 3.7 fusion.64
  377.5 3.0 convolution_convert_fusion.1
  380.6 33.4 %all_to_all.15 = bf16[32,64,512]{2,1,0:T(8,128)(2,1)S(1)} all-to-all(bf16[32,64,512]{2,1,0:T(8,128)(2,1)S(1)} %bitcast.61), channel_id=1, replica_groups=mesh['probe'=4,'fsdp'=32] {'fsdp'}, dimensions={0} | all-to-all | bytes 4194304 | tf_op jit(solution)/shard_map/all_to_all | solution.py:29
  414.9 29.9 %all-to-all-start.1 = ((bf16[4,64,128]{2,1,0:T(8,128)(2,1)}), bf16[4,64,128]{2,1,0:T(8,128)(2,1)S(1)}, u32[]{:S(2)}, u32[]{:S(2)}) async-start(bf16[4,64,128]{2,1,0:T(8,128)(2,1)} %copy.63), calls=%async_computation.1 | async-start | bytes 131072 | tf_op jit(solution)/shard_map/all_to_all | solution.py:29
  444.8 102.9 %reduce-scatter.2.cloned.1.call-done = bf16[64,2048]{1,0:T(8,128)(2,1)} async-done(((bf16[2048,2048]{1,0:T(8,128)(2,1)}), bf16[64,2048]{1,0:T(8,128)(2,1)}) %reduce-scatter.2.cloned.1.call-update) | async-done | bytes 262160 | tf_op jit(solution)/shard_map/reduce_scatter | solution.py:160
  549.4 28.3 %all-to-all-start.2 = ((bf16[4,64,512]{2,1,0:T(8,128)(2,1)}), bf16[4,64,512]{2,1,0:T(8,128)(2,1)S(1)}, u32[]{:S(2)}, u32[]{:S(2)}) async-start(bf16[4,64,512]{2,1,0:T(8,128)(2,1)} %bitcast.58), calls=%async_computation.3 | async-start | bytes 524288 | tf_op jit(solution)/shard_map/all_to_all | solution.py:29
  578.3 5.9 %all-to-all-done.2 = bf16[4,64,512]{2,1,0:T(8,128)(2,1)S(1)} async-done(((bf16[4,64,512]{2,1,0:T(8,128)(2,1)}), bf16[4,64,512]{2,1,0:T(8,128)(2,1)S(1)}, u32[]{:S(2)}, u32[]{:S(2)}) %all-to-all-start.2) | async-done | bytes 262176 | tf_op jit(solution)/shard_map/all_to_all | solution.py:29
  (54 shorter events, 31.3 us)
Async XLA Ops:
  7.2 161.7 %all-gather.3.cloned.1.call-start = ((), (), s32[]{:S(2)}) async-start(), calls=%async_computation.4 | async-start | bytes 12976128 | tf_op jit(solution)/shard_map/all_gather | solution.py:14
  9.0 324.4 %all-gather.5.cloned.1.call-start = ((), (), s32[]{:S(2)}) async-start(), calls=%async_computation.5 | async-start | bytes 8650752 | tf_op jit(solution)/shard_map/all_gather | solution.py:144
  9.8 537.9 %reduce-scatter.2.cloned.1.call-start = ((), (), s32[]{:S(2)}) async-start(), calls=%async_computation.6 | async-start | bytes 8650752 | tf_op jit(solution)/shard_map/reduce_scatter | solution.py:160
  13.3 155.6 %copy-start.2 = (bf16[512,2048]{1,0:T(8,128)(2,1)S(1)}, bf16[512,2048]{1,0:T(8,128)(2,1)}, u32[]{:S(2)}) copy-start(bf16[512,2048]{1,0:T(8,128)(2,1)} %param.7) | copy-start | bytes 6291460
  186.8 2.2 copy-start.1
  198.1 3.1 copy-start.5
  199.3 2.0 copy-start
  202.0 7.6 %copy-start.4 = (bf16[2,256,4,128]{3,2,1,0:T(4,128)(2,1)S(1)}, bf16[2,256,4,128]{3,2,1,0:T(4,128)(2,1)}, u32[]{:S(2)}) copy-start(bf16[2,256,4,128]{3,2,1,0:T(4,128)(2,1)} %reshape.128) | copy-start | bytes 1572868
  220.2 121.0 %copy-start.3 = (bf16[512,2048]{1,0:T(8,128)(2,1)S(1)}, bf16[512,2048]{1,0:T(8,128)(2,1)}, u32[]{:S(2)}) copy-start(bf16[512,2048]{1,0:T(8,128)(2,1)} %convert_element_type.143) | copy-start | bytes 6291460
  351.2 1.3 copy-start.6
  359.4 1.6 copy-start.7
  414.9 134.5 %all-to-all-start.1 = ((bf16[4,64,128]{2,1,0:T(8,128)(2,1)}), bf16[4,64,128]{2,1,0:T(8,128)(2,1)S(1)}, u32[]{:S(2)}, u32[]{:S(2)}) async-start(bf16[4,64,128]{2,1,0:T(8,128)(2,1)} %copy.63), calls=%async_computation.1 | async-start | bytes 131072 | tf_op jit(solution)/shard_map/all_to_all | solution.py:29
  549.4 34.8 %all-to-all-start.2 = ((bf16[4,64,512]{2,1,0:T(8,128)(2,1)}), bf16[4,64,512]{2,1,0:T(8,128)(2,1)S(1)}, u32[]{:S(2)}, u32[]{:S(2)}) async-start(bf16[4,64,512]{2,1,0:T(8,128)(2,1)} %bitcast.58), calls=%async_computation.3 | async-start | bytes 524288 | tf_op jit(solution)/shard_map/all_to_all | solution.py:29
Sparse Core Ops, SparseCore 0:
  9.6 159.1 all-gather.2
  170.5 162.9 all-gather.4
  359.5 188.1 reduce-scatter.1
where the time goes:
time: 597 us; the launch traced here: 592 us
  waiting for transfers between devices  371 us (62%)
  matrix products  63.9 us (11%)
  starting transfers between devices  58.3 us (10%)
  local copies, waits for them, and re-layouts  34.3 us (6%)
  blocking collectives  33.4 us (6%)
  other arithmetic  15.4 us (3%)
  between operations  14.9 us (2%)
    all_gather x1, waiting for transfers between devices, in_one_piece(): lax.all_gather(both, axis, axis=dim, tiled=True)  149 us
    all_gather x1, waiting for transfers between devices, body(): whole_out = lax.all_gather(output_weight, 'fsdp', axis=0, tiled=True)  113 us
    reduce_scatter x1, waiting for transfers between devices, body(): lax.psum_scatter(lax.dot_general(portion, cotangent, contract_rows, prefe...  103 us
    all_to_all x2, starting transfers between devices, sent_and_summed(): parts = lax.all_to_all(split_up(value, dim, size), axis, 0, 0, tiled=True)  58.2 us
    all_to_all x1, blocking collectives, sent_and_summed(): parts = lax.all_to_all(split_up(value, dim, size), axis, 0, 0, tiled=True)  33.4 us
  transfers between devices with their start and end apart: 5, of which 4 were waited for; matrix products, arithmetic and copies ran while one was open for 14% of the time, Pallas kernels for 0%

commit v1 on v0

--- a/solution.py
+++ b/solution.py
@@ -141,7 +141,9 @@
     probe_part = jnp.dot(context, signs_out, preferred_element_type=jnp.float32) * query_width ** (
         -0.5
     )
-    whole_out = lax.all_gather(output_weight, "fsdp", axis=0, tiled=True)
+    whole_out = jnp.concatenate(
+        lax.all_to_all(jnp.stack([output_weight] * lax.axis_size("fsdp")), "fsdp", 0, 0), axis=0
+    )
     forward_part = jnp.dot(tangent_context, whole_out, preferred_element_type=jnp.float32)
     cotangent = (forward_part + probe_part).astype(jnp.bfloat16)
     back_context = lax.dot_general(

time: 597 us -> 580 us (0.972)
  waiting for transfers between devices: 371 us -> 356 us
  blocking collectives: 33.4 us -> 41.2 us
  starting transfers between devices: 58.3 us -> 50.7 us
    all_gather x1 -> x0, waiting for transfers between devices: 113 us -> none  [body(): whole_out = lax.all_gather(output_weight, 'fsdp', axis=0, tiled=True)]
    all_gather x1, waiting for transfers between devices: 149 us -> 246 us  [in_one_piece(): lax.all_gather(both, axis, axis=dim, tiled=True)]
    all_to_all x2, starting transfers between devices: 58.2 us -> 41.1 us  [sent_and_summed(): parts = lax.all_to_all(split_up(value, dim, size), axis, 0, 0, tiled=True)]
    all_to_all x0 -> x1, starting transfers between devices: none -> 9.47 us  [body(): lax.all_to_all(jnp.stack([output_weight] * lax.axis_size('fsdp')), 'fsdp'...]
    all_to_all x1, blocking collectives: 33.4 us -> 41.2 us  [sent_and_summed(): parts = lax.all_to_all(split_up(value, dim, size), axis, 0, 0, tiled=True)]
  transfers between devices with their start and end apart: 5 -> 5, of which waited for: 4 -> 3; matrix products, arithmetic and copies ran while one was open for 14% -> 14% of each run, Pallas kernels for 0% -> 0%
where the time goes in v1:
time: 580 us; the launch traced here: 573 us
  waiting for transfers between devices  356 us (61%)
  matrix products  61.4 us (11%)
  starting transfers between devices  50.7 us (9%)
  blocking collectives  41.2 us (7%)
  local copies, waits for them, and re-layouts  35.4 us (6%)
  between operations  15.2 us (3%)
  other arithmetic  13.1 us (2%)
    all_gather x1, waiting for transfers between devices, in_one_piece(): lax.all_gather(both, axis, axis=dim, tiled=True)  246 us
    reduce_scatter x1, waiting for transfers between devices, body(): lax.psum_scatter(lax.dot_general(portion, cotangent, contract_rows, prefe...  104 us
    all_to_all x1, blocking collectives, sent_and_summed(): parts = lax.all_to_all(split_up(value, dim, size), axis, 0, 0, tiled=True)  41.2 us
    all_to_all x2, starting transfers between devices, sent_and_summed(): parts = lax.all_to_all(split_up(value, dim, size), axis, 0, 0, tiled=True)  41.1 us
  transfers between devices with their start and end apart: 5, of which 3 were waited for; matrix products, arithmetic and copies ran while one was open for 14% of the time, Pallas kernels for 0%

profile of v1, /device:TPU:1, one launch (start us, length us, event | category | flops | bytes accessed | tf_op | source)
XLA Modules:
  0.0 573.4 jit_solution(13524223194545491153)
XLA Ops:
  9.0 5.3 stack.2
  14.3 9.5 %all-to-all-start = ((bf16[32,64,2048]{2,1,0:T(8,128)(2,1)}), bf16[32,64,2048]{2,1,0:T(8,128)(2,1)}, u32[]{:S(2)}, u32[]{:S(2)}) async-start(bf16[32,64,2048]{2,1,0:T(8,128)(2,1)} %stack.2), calls=%async_computation | async-start | bytes 16777216 | tf_op jit(solution)/shard_map/all_to_all | solution.py:145
  25.0 3.1 fusion.63
  30.2 246.3 %all-gather.2.cloned.1.call-done = bf16[2048,3072]{1,0:T(8,128)(2,1)} async-done(((bf16[64,3072]{1,0:T(8,128)(2,1)}), bf16[2048,3072]{1,0:T(8,128)(2,1)}) %all-gather.2.cloned.1.call-update) | async-done | bytes 12582928 | tf_op jit(solution)/shard_map/all_gather | solution.py:14
  276.5 2.9 fusion.57
  280.3 7.1 %fusion.30 = f32[64,8,16,128]{3,1,2,0:T(8,128)S(1)} fusion(bf16[2048,3072]{1,0:T(8,128)(2,1)} %all-gather.2.cloned.1.call-done, bf16[512,2048]{1,0:T(8,128)(2,1)S(1)} %copy-done.2, f32[2048]{0:T(1024)S(1)} %convert_element_type.128, f32[512]{0:T(512)S(1)} %add_rsqrt_fusion), kind=kOutput, calls=%fused_computation.49 | convolution fusion | flops 4299161600 | bytes 14690304 | tf_op jit(solution)/shard_map/dot_general | solution.py:127
  290.3 3.0 fusion.36
  309.2 3.1 copy.59
  312.3 4.5 convert_element_type.143
  316.8 3.0 convert_bitcast_fusion.1
  319.8 3.1 copy.56
  322.8 3.3 convert_element_type.139
  326.2 7.4 %fusion.104 = f32[512,2048]{1,0:T(8,128)S(1)} fusion(bf16[512,2048]{1,0:T(8,128)(2,1)S(1)} %convert_element_type.139, bf16[2048,2048]{1,0:T(8,128)(2,1)} %bitcast.8), kind=kOutput, calls=%fused_computation.127 | convolution fusion | flops 4294967296 | bytes 14680064 | tf_op jit(solution)/shard_map/dot_general | solution.py:147
  333.6 10.0 %add_convert_fusion = bf16[512,2048]{1,0:T(8,128)(2,1)S(1)} fusion(f32[512,2048]{1,0:T(8,128)S(1)} %fusion.104, bf16[512,2048]{1,0:T(8,128)(2,1)S(1)} %copy-done.3, s32[]{:T(128)S(6)} %add.79, s32[2048]{0:T(1024)S(1)} %iota_multiply_fusion), kind=kOutput, calls=%fused_computation.40 | convolution fusion | flops 4361027584 | bytes 8396804 | tf_op jit(solution)/shard_map/dot_general | solution.py:141
  343.6 6.8 %convolution_convert_fusion = bf16[2048,2048]{1,0:T(8,128)(2,1)} fusion(bf16[512,2048]{1,0:T(8,128)(2,1)S(1)} %copy-done.3, bf16[512,2048]{1,0:T(8,128)(2,1)S(1)} %add_convert_fusion), kind=kOutput, calls=%fused_computation.26 | convolution fusion | flops 4299161600 | bytes 12582912 | tf_op jit(solution)/shard_map/dot_general | solution.py:163
  350.5 9.3 %convolution_convert_fusion.2 = bf16[512,2048]{1,0:T(8,128)(2,1)} fusion(bf16[512,2048]{1,0:T(8,128)(2,1)S(1)} %add_convert_fusion, bf16[2048,2048]{1,0:T(8,128)(2,1)} %bitcast.8), kind=kOutput, calls=%fused_computation.48 | convolution fusion | flops 4296015872 | bytes 12582912 | tf_op jit(solution)/shard_map/dot_general | solution.py:149
  359.8 3.2 reshape.138
  363.0 3.7 fusion.64
  367.0 3.0 convolution_convert_fusion.1
  370.0 41.2 %all_to_all.20 = bf16[32,64,512]{2,1,0:T(8,128)(2,1)S(1)} all-to-all(bf16[32,64,512]{2,1,0:T(8,128)(2,1)S(1)} %bitcast.62), channel_id=1, replica_groups=mesh['probe'=4,'fsdp'=32] {'fsdp'}, dimensions={0} | all-to-all | bytes 4194304 | tf_op jit(solution)/shard_map/all_to_all | solution.py:29
  412.1 14.9 %all-to-all-start.2 = ((bf16[4,64,128]{2,1,0:T(8,128)(2,1)}), bf16[4,64,128]{2,1,0:T(8,128)(2,1)S(1)}, u32[]{:S(2)}, u32[]{:S(2)}) async-start(bf16[4,64,128]{2,1,0:T(8,128)(2,1)} %copy.63), calls=%async_computation.2 | async-start | bytes 131072 | tf_op jit(solution)/shard_map/all_to_all | solution.py:29
  427.1 104.2 %reduce-scatter.2.cloned.1.call-done = bf16[64,2048]{1,0:T(8,128)(2,1)} async-done(((bf16[2048,2048]{1,0:T(8,128)(2,1)}), bf16[64,2048]{1,0:T(8,128)(2,1)}) %reduce-scatter.2.cloned.1.call-update) | async-done | bytes 262160 | tf_op jit(solution)/shard_map/reduce_scatter | solution.py:162
  532.9 26.2 %all-to-all-start.3 = ((bf16[4,64,512]{2,1,0:T(8,128)(2,1)}), bf16[4,64,512]{2,1,0:T(8,128)(2,1)S(1)}, u32[]{:S(2)}, u32[]{:S(2)}) async-start(bf16[4,64,512]{2,1,0:T(8,128)(2,1)} %bitcast.59), calls=%async_computation.4 | async-start | bytes 524288 | tf_op jit(solution)/shard_map/all_to_all | solution.py:29
  559.8 5.9 %all-to-all-done.3 = bf16[4,64,512]{2,1,0:T(8,128)(2,1)S(1)} async-done(((bf16[4,64,512]{2,1,0:T(8,128)(2,1)}), bf16[4,64,512]{2,1,0:T(8,128)(2,1)S(1)}, u32[]{:S(2)}, u32[]{:S(2)}) %all-to-all-start.3) | async-done | bytes 262176 | tf_op jit(solution)/shard_map/all_to_all | solution.py:29
  (52 shorter events, 28.3 us)
Async XLA Ops:
  7.2 269.3 %all-gather.2.cloned.1.call-start = ((), (), s32[]{:S(2)}) async-start(), calls=%async_computation.5 | async-start | bytes 12976128 | tf_op jit(solution)/shard_map/all_gather | solution.py:14
  14.3 10.2 %copy-start.6 = (bf16[2048]{0:T(1024)(128)(2,1)S(1)}, bf16[2048]{0:T(1024)(128)(2,1)}, u32[]{:S(2)}) copy-start(bf16[2048]{0:T(1024)(128)(2,1)} %param.8) | copy-start | bytes 12292
  14.3 10.2 %copy-start.2 = (bf16[512,2048]{1,0:T(8,128)(2,1)S(1)}, bf16[512,2048]{1,0:T(8,128)(2,1)}, u32[]{:S(2)}) copy-start(bf16[512,2048]{1,0:T(8,128)(2,1)} %param.7) | copy-start | bytes 6291460
  14.3 311.8 %all-to-all-start = ((bf16[32,64,2048]{2,1,0:T(8,128)(2,1)}), bf16[32,64,2048]{2,1,0:T(8,128)(2,1)}, u32[]{:S(2)}, u32[]{:S(2)}) async-start(bf16[32,64,2048]{2,1,0:T(8,128)(2,1)} %stack.2), calls=%async_computation | async-start | bytes 16777216 | tf_op jit(solution)/shard_map/all_to_all | solution.py:145
  23.8 507.4 %reduce-scatter.2.cloned.1.call-start = ((), (), s32[]{:S(2)}) async-start(), calls=%async_computation.6 | async-start | bytes 8650752 | tf_op jit(solution)/shard_map/reduce_scatter | solution.py:162
  294.0 2.2 copy-start.1
  305.4 3.1 copy-start.5
  306.5 1.9 copy-start
  309.2 7.5 %copy-start.4 = (bf16[2,256,4,128]{3,2,1,0:T(4,128)(2,1)S(1)}, bf16[2,256,4,128]{3,2,1,0:T(4,128)(2,1)}, u32[]{:S(2)}) copy-start(bf16[2,256,4,128]{3,2,1,0:T(4,128)(2,1)} %reshape.133) | copy-start | bytes 1572868
  326.1 7.5 %copy-start.3 = (bf16[512,2048]{1,0:T(8,128)(2,1)S(1)}, bf16[512,2048]{1,0:T(8,128)(2,1)}, u32[]{:S(2)}) copy-start(bf16[512,2048]{1,0:T(8,128)(2,1)} %convert_element_type.143) | copy-start | bytes 6291460
  412.1 120.8 %all-to-all-start.2 = ((bf16[4,64,128]{2,1,0:T(8,128)(2,1)}), bf16[4,64,128]{2,1,0:T(8,128)(2,1)S(1)}, u32[]{:S(2)}, u32[]{:S(2)}) async-start(bf16[4,64,128]{2,1,0:T(8,128)(2,1)} %copy.63), calls=%async_computation.2 | async-start | bytes 131072 | tf_op jit(solution)/shard_map/all_to_all | solution.py:29
  532.9 32.8 %all-to-all-start.3 = ((bf16[4,64,512]{2,1,0:T(8,128)(2,1)}), bf16[4,64,512]{2,1,0:T(8,128)(2,1)S(1)}, u32[]{:S(2)}, u32[]{:S(2)}) async-start(bf16[4,64,512]{2,1,0:T(8,128)(2,1)} %bitcast.59), calls=%async_computation.4 | async-start | bytes 524288 | tf_op jit(solution)/shard_map/all_to_all | solution.py:29
Sparse Core Ops, SparseCore 0:
  9.6 266.7 all-gather.1
  350.6 180.6 reduce-scatter.1
